TPU v7x, 128 devices: a whole 4x4x4 slice. The times are simulated.
128 devices in a mesh: dp: 8 (over y, core), tensor: 16 (over x, z).
Axes of the slice: x: 4, y: 4, z: 4, core: 2. Of those that a mesh axis runs over, the one named last changes fastest.
Arguments:
- inputs: bfloat16 [24576, 5120], P('dp', 'tensor'), may hold values from -6 to 6
- cotangent: bfloat16 [24576, 4096], P('dp', 'tensor'), may hold values from -192 to 192
- lengths: int32 [64], P('dp'), may hold values from 96 to 384
- momentum: float32 [8, 4096, 5120], P('dp', 'tensor'), may hold values from -26 to 26
- weight: bfloat16 [4096, 5120], P('tensor'), may hold values from -0.00039863586 to 0.00039863586
- right_factor: float32 [5120, 64], replicated, may hold values from -1 to 1
Outputs:
- new_weight: bfloat16 [4096, 5120], P('tensor')
- new_momentum: float32 [8, 4096, 5120], P('dp', 'tensor')
- new_right: float32 [5120, 64], replicated
Inputs may be any that keep to these rules, and one draw needn't show every extreme that they name: The first lengths[i] positions of block i are real tokens, the rest padding.
All inputs are finite; a program needn't handle non-finite values.
Results may differ from a plain program's by a relative error of at most 0.00045.
Values may be sent and summed in bfloat16 or wider, within the bound.
A program may use at most 128 MiB of HBM per device.

v0:
```python
import math
import jax
import jax.numpy as jnp
from jax import lax
from jax.sharding import PartitionSpec as P

EPS = 1e-06
MU = 0.95
LR = 0.02


def from_everyone(x, axis):
    devices = lax.axis_size(axis)
    return lax.all_to_all(jnp.broadcast_to(x[None], (devices, *x.shape)), axis, 0, 0, tiled=True)


def over_copies(x, axis):
    return from_everyone(x, axis).sum(axis=0)


def per_device(inputs, cotangent, lengths, momentum, weight, right_factor):
    hi = lax.Precision.HIGHEST
    contract = (((0,), (0,)), ((), ()))
    replicas = lax.axis_size("dp")
    block_len = inputs.shape[0] // lengths.shape[0]
    position = jnp.arange(block_len, dtype=jnp.int32)
    keep = (position[None, :] < lengths[:, None]).reshape(-1).astype(jnp.bfloat16)
    masked = inputs * keep[:, None]
    count = jnp.sum(lengths.astype(jnp.float32))
    grad = lax.dot_general(
        cotangent,
        lax.all_gather(masked, "tensor", axis=1, tiled=True),
        contract,
        preferred_element_type=jnp.float32,
    )
    both = momentum[0] + grad / count
    left = over_copies(jnp.dot(both, right_factor, precision=hi), "dp") / replicas
    gram = over_copies(jnp.dot(left.T, left, precision=hi), "tensor")
    factor = jnp.linalg.cholesky(gram)
    ortho = jax.scipy.linalg.solve_triangular(factor, left.T, lower=True).T
    term = lax.dot_general(both, ortho, contract, precision=hi) / replicas
    right = lax.psum(term, ("dp", "tensor"))
    squares = jnp.sum(right * right, axis=0)
    new_right = right * lax.rsqrt(squares + EPS)
    lowrank = jnp.dot(ortho, right.T, precision=hi)
    new_momentum = (both - (1.0 - MU) * lowrank)[None]
    rows_all = ortho.shape[0] * lax.axis_size("tensor")
    update = jnp.dot(ortho, new_right.T, precision=hi)
    new_weight = (
        weight.astype(jnp.float32) - LR * math.sqrt(rows_all / right.shape[0]) * update
    ).astype(jnp.bfloat16)
    return (new_weight, new_momentum, new_right)


def solution(mesh):
    placed = (
        P("dp", "tensor"),
        P("dp", "tensor"),
        P("dp"),
        P("dp", "tensor", None),
        P("tensor", None),
        P(),
    )
    return jax.shard_map(
        per_device,
        mesh=mesh,
        in_specs=placed,
        out_specs=(P("tensor", None), P("dp", "tensor", None), P()),
        check_vma=False,
    )
```

profile of v0, /device:TPU:1, one launch (start us, length us, event | category | flops | bytes accessed | tf_op | source)
XLA Modules:
  0.0 449.7 jit_solution(14454124653131563446)
XLA Ops:
  7.2 0.0 all-gather.2.cloned.1.call-start
  7.2 0.8 fusion.15
  8.1 3.0 broadcast_multiply_fusion
  11.0 0.0 all-gather.2.cloned.1.call-update
  11.1 0.0 all-reduce.2.cloned.1.call-start
  11.1 5.9 %copy.22 = f32[1,256,5120]{1,2,0:T(8,128)} copy(f32[1,256,5120]{2,1,0:T(8,128)} %param.9) | data formatting | bytes 10485760 | tf_op args[3]
  17.0 0.6 convert_reduce_fusion
  17.6 183.0 %all-gather.2.cloned.1.call-done = bf16[3072,5120]{0,1:T(8,128)(2,1)} async-done(((bf16[3072,320]{0,1:T(8,128)(2,1)}), bf16[3072,5120]{0,1:T(8,128)(2,1)}) %all-gather.2.cloned.1.call-update) | async-done | bytes 31457296 | tf_op jit(solution)/shard_map/all_gather | solution.py:32
  200.6 17.1 %fusion.5 = f32[256,5120]{0,1:T(8,128)S(1)} fusion(bf16[3072,5120]{0,1:T(8,128)(2,1)} %all-gather.2.cloned.1.call-done, bf16[3072,256]{1,0:T(8,128)(2,1)S(1)} %copy-done, f32[1,256,5120]{1,2,0:T(8,128)} %copy.22, f32[]{:T(128)} %convert_reduce_fusion), kind=kOutput, calls=%fused_computation.8 | convolution fusion | flops 8055685120 | bytes 43515908 | tf_op jit(solution)/shard_map/dot_general | solution.py:30
  217.7 3.2 fusion.18
  221.0 14.2 %all_to_all.10 = f32[8,256,64]{1,2,0:T(8,128)S(1)} all-to-all(f32[8,256,64]{1,2,0:T(8,128)S(1)} %broadcast_in_dim.7), channel_id=1, replica_groups=mesh['dp'=8,'tensor'=16] {'dp'}, dimensions={0} | all-to-all | bytes 1048576 | tf_op jit(solution)/shard_map/all_to_all | solution.py:14
  235.2 0.2 fusion.8
  235.5 0.3 reshape.40
  235.8 12.2 %all_to_all.11 = f32[16,1,4096]{2,1,0:T(1,128)S(1)} all-to-all(f32[16,1,4096]{2,1,0:T(1,128)S(1)} %reshape.40), channel_id=1, replica_groups=mesh['dp'=8,'tensor'=16] {'tensor'}, dimensions={0} | all-to-all | bytes 524288 | tf_op jit(solution)/shard_map/all_to_all | solution.py:14
  248.1 0.5 broadcast.66
  248.6 1.3 reduce.6
  249.8 0.2 reshape.41
  250.1 0.1 copy.23
  250.2 5.8 %cholesky.16 = f32[64,64]{1,0:T(8,128)S(1)} custom-call(f32[64,64]{1,0:T(8,128)S(1)} %fusion.12), custom_call_target="Cholesky" | custom-call | tf_op jit(solution)/shard_map/jit(cholesky)/cholesky | solution.py:39
  256.1 0.6 compare_reduce_fusion
  256.7 0.7 fusion.10
  257.4 4.9 %custom-call.7 = f32[1,64,64]{1,2,0:T(8,128)S(1)} custom-call(f32[1,64,64]{2,1,0:T(8,128)S(1)} %fusion.10), custom_call_target="InvertDiagBlocksLowerTriangular" | custom-call | tf_op jit(solution)/shard_map/jit(_solve_triangular)/triangular_solve | solution.py:40
  262.3 0.3 fusion.6
  262.6 8.7 %convolution_multiply_fusion.2 = f32[5120,64]{0,1:T(8,128)} fusion(f32[256,5120]{0,1:T(8,128)} %copy-done.2, f32[64,256]{1,0:T(8,128)S(1)} %fusion.6), kind=kOutput, calls=%fused_computation.9 | convolution fusion | flops 1006960640 | bytes 6619136 | tf_op jit(solution)/shard_map/dot_general | solution.py:41
  271.3 0.0 all-reduce.2.cloned.1.call-update
  271.3 146.8 %all-reduce.2.cloned.1.call-done = f32[5120,64]{0,1:T(8,128)} async-done(((f32[5120,64]{0,1:T(8,128)}), f32[5120,64]{0,1:T(8,128)}) %all-reduce.2.cloned.1.call-update) | async-done | bytes 1310736 | tf_op jit(solution)/shard_map/psum | solution.py:42
  418.1 1.5 multiply_reduce_fusion
  419.6 9.7 %fusion.2 = f32[1,256,5120]{1,2,0:T(8,128)} fusion(f32[256,5120]{0,1:T(8,128)} %copy-done.2, f32[64,256]{1,0:T(8,128)S(1)} %fusion.6, f32[5120,64]{0,1:T(8,128)} %all-reduce.2.cloned.1.call-done), kind=kOutput, calls=%fused_computation.4 | convolution fusion | flops 1009254400 | bytes 11862016 | tf_op jit(solution)/shard_map/dot_general | solution.py:45
  429.3 6.0 %copy.25 = f32[1,256,5120]{2,1,0:T(8,128)} copy(f32[1,256,5120]{1,2,0:T(8,128)} %fusion.2) | data formatting | bytes 10485760
  435.3 0.2 broadcast_multiply_fusion.1
  435.5 1.6 copy-done.5
  437.1 5.8 %fusion.3 = bf16[256,5120]{1,0:T(8,128)(2,1)} fusion(f32[64,256]{1,0:T(8,128)S(1)} %fusion.6, f32[5120,64]{0,1:T(8,128)S(1)} %broadcast_multiply_fusion.1, bf16[256,5120]{1,0:T(8,128)(2,1)S(1)} %copy-done.5), kind=kOutput, calls=%fused_computation.5 | convolution fusion | flops 1011875840 | bytes 6619136 | tf_op jit(solution)/shard_map/dot_general | solution.py:48
  (23 shorter events, 0.3 us)
Async XLA Ops:
  7.2 193.5 %copy-start = (bf16[3072,256]{1,0:T(8,128)(2,1)S(1)}, bf16[3072,256]{1,0:T(8,128)(2,1)}, u32[]{:S(2)}) copy-start(bf16[3072,256]{1,0:T(8,128)(2,1)} %param.7) | copy-start | bytes 4718596
  7.2 193.5 %all-gather.2.cloned.1.call-start = ((), (), s32[]{:S(2)}) async-start(), calls=%async_computation.2 | async-start | bytes 33423360 | tf_op jit(solution)/shard_map/all_gather | solution.py:32
  11.1 5.9 %copy-start.7 = (s32[8]{0:T(128)S(1)}, s32[8]{0:T(128)}, u32[]{:S(2)}) copy-start(s32[8]{0:T(128)} %param.8) | copy-start | bytes 100
  11.1 407.0 %all-reduce.2.cloned.1.call-start = ((), (), s32[]{:S(2)}) async-start(), calls=%async_computation.3 | async-start | bytes 2621440 | tf_op jit(solution)/shard_map/psum | solution.py:42
  17.6 200.1 %copy-start.6 = (f32[5120,64]{0,1:T(8,128)S(1)}, f32[5120,64]{0,1:T(8,128)}, u32[]{:S(2)}) copy-start(f32[5120,64]{0,1:T(8,128)} %param.11) | copy-start | bytes 3932164
  217.7 3.2 copy-start.2
  429.3 6.0 %copy-start.3 = (f32[5120,64]{0,1:T(8,128)S(1)}, f32[5120,64]{0,1:T(8,128)}, u32[]{:S(2)}) copy-start(f32[5120,64]{0,1:T(8,128)} %all-reduce.2.cloned.1.call-done) | copy-start | bytes 3932164
  435.3 1.7 copy-start.5
  435.3 7.6 %copy-start.1 = (bf16[3072,256]{1,0:T(8,128)(2,1)S(1)}, bf16[3072,256]{1,0:T(8,128)(2,1)}, u32[]{:S(2)}) copy-start(bf16[3072,256]{1,0:T(8,128)(2,1)} %param.7) | copy-start | bytes 4718596
  437.1 5.8 %copy-start.4 = (f32[5120,64]{0,1:T(8,128)}, f32[5120,64]{0,1:T(8,128)S(1)}, u32[]{:S(2)}) copy-start(f32[5120,64]{0,1:T(8,128)S(1)} %broadcast_multiply_fusion.1) | copy-start | bytes 3932164
Sparse Core Ops, SparseCore 0:
  11.2 189.4 all-gather.1
  271.4 146.6 all-reduce.1
where the time goes:
time: 450 us
  waiting for transfers between devices  330 us (73%)
  matrix products  44.9 us (10%)
  blocking collectives  26.5 us (6%)
  other arithmetic  19.5 us (4%)
  local copies, waits for them, and re-layouts  14.7 us (3%)
  between operations  14.2 us (3%)
    all_gather x1, waiting for transfers between devices, per_device(): lax.all_gather(masked, 'tensor', axis=1, tiled=True)  183 us
    psum x1, waiting for transfers between devices, per_device(): right = lax.psum(term, ('dp', 'tensor'))  147 us
    all_to_all x2, blocking collectives, from_everyone(): lax.all_to_all(jnp.broadcast_to(x[None], (devices, *x.shape)), axis, 0, 0...  26.5 us
    dot_general x1, matrix products, per_device(): lax.dot_general(cotangent, lax.all_gather(masked, 'tensor', axis=1, tiled...  17.1 us
    unnamed x20, local copies, waits for them, and re-layouts  14 us
    dot_general x1, matrix products, per_device(): lowrank = jnp.dot(ortho, right.T, precision=hi)  9.69 us
  transfers between devices with their start and end apart: 2, of which 2 were waited for; matrix products, arithmetic and copies ran while one was open for 1% of the time, Pallas kernels for 0%

commit v1 on v0

--- a/solution.py
+++ b/solution.py
@@ -29,7 +29,15 @@
     count = jnp.sum(lengths.astype(jnp.float32))
     grad = lax.dot_general(
         cotangent,
-        lax.all_gather(masked, "tensor", axis=1, tiled=True),
+        jnp.concatenate(
+            jax.lax.all_to_all(
+                jnp.stack([masked for _ in range(jax.lax.psum(1, axis_name="tensor"))]),
+                "tensor",
+                0,
+                0,
+            ),
+            axis=1,
+        ),
         contract,
         preferred_element_type=jnp.float32,
     )

time: 450 us -> 863 us (1.92)
  waiting for transfers between devices: 330 us -> 720 us
  local copies, waits for them, and re-layouts: 14.7 us -> 25.1 us
    all_to_all x0 -> x1, waiting for transfers between devices: none -> 573 us  [per_device(): jax.lax.all_to_all(jnp.stack([masked for _ in range(jax.lax.psum(1, axis_...]
    all_gather x1 -> x0, waiting for transfers between devices: 183 us -> none  [per_device(): lax.all_gather(masked, 'tensor', axis=1, tiled=True)]
    another operation x0 -> x1, local copies, waits for them, and re-layouts: none -> 10.6 us  [per_device(): jnp.stack([masked for _ in range(jax.lax.psum(1, axis_name='tensor'))])]
where the time goes in v1:
time: 863 us; the launch traced here: 862 us
  waiting for transfers between devices  720 us (83%)
  matrix products  45 us (5%)
  blocking collectives  32.3 us (4%)
  local copies, waits for them, and re-layouts  25.1 us (3%)
  other arithmetic  16.9 us (2%)
  between operations  14.2 us (2%)
    all_to_all x1, waiting for transfers between devices, per_device(): jax.lax.all_to_all(jnp.stack([masked for _ in range(jax.lax.psum(1, axis_...  573 us
    psum x1, waiting for transfers between devices, per_device(): right = lax.psum(term, ('dp', 'tensor'))  147 us
    all_to_all x2, blocking collectives, from_everyone(): lax.all_to_all(jnp.broadcast_to(x[None], (devices, *x.shape)), axis, 0, 0...  32.3 us
  transfers between devices with their start and end apart: 2, of which 2 were waited for; matrix products, arithmetic and copies ran while one was open for 1% of the time, Pallas kernels for 0%

profile of v1, /device:TPU:1, one launch (start us, length us, event | category | flops | bytes accessed | tf_op | source)
XLA Modules:
  0.0 862.0 jit_solution(2959048698053935739)
XLA Ops:
  7.2 0.8 fusion.15
  8.0 1.7 broadcast_multiply_fusion
  9.7 10.6 %stack.2 = bf16[16,3072,320]{1,2,0:T(8,128)(2,1)} broadcast(bf16[3072,320]{0,1:T(8,128)(2,1)S(1)} %broadcast_multiply_fusion), dimensions={1,2} | broadcast | bytes 33423360 | tf_op jit(solution)/shard_map/stack | solution.py:34
  20.4 8.5 all-to-all-start
  28.8 0.0 all-reduce.2.cloned.1.call-start
  28.9 5.9 copy.28
  34.8 0.6 convert_reduce_fusion
  35.4 573.2 %all-to-all-done = bf16[16,3072,320]{1,2,0:T(8,128)(2,1)} async-done(((bf16[16,3072,320]{1,2,0:T(8,128)(2,1)}), bf16[16,3072,320]{1,2,0:T(8,128)(2,1)}, u32[]{:S(2)}, u32[]{:S(2)}) %all-to-all-start) | async-done | bytes 31457312 | tf_op jit(solution)/shard_map/all_to_all | solution.py:33
  608.5 17.1 %fusion.5 = f32[256,5120]{0,1:T(8,128)S(1)} fusion(bf16[3072,5120]{0,1:T(8,128)(2,1)} %bitcast.2, bf16[3072,256]{1,0:T(8,128)(2,1)S(1)} %copy-done, f32[1,256,5120]{1,2,0:T(8,128)} %copy.28, f32[]{:T(128)} %convert_reduce_fusion), kind=kOutput, calls=%fused_computation.8 | convolution fusion | flops 8055685120 | bytes 43515908 | tf_op jit(solution)/shard_map/dot_general | solution.py:30
  625.7 3.2 fusion.18
  628.9 15.1 %all_to_all.15 = f32[8,256,64]{1,2,0:T(8,128)S(1)} all-to-all(f32[8,256,64]{1,2,0:T(8,128)S(1)} %broadcast_in_dim.7), channel_id=1, replica_groups=mesh['dp'=8,'tensor'=16] {'dp'}, dimensions={0} | all-to-all | bytes 1048576 | tf_op jit(solution)/shard_map/all_to_all | solution.py:14
  644.1 0.2 fusion.8
  644.3 0.3 reshape.50
  644.7 17.2 %all_to_all.16 = f32[16,1,4096]{2,1,0:T(1,128)S(1)} all-to-all(f32[16,1,4096]{2,1,0:T(1,128)S(1)} %reshape.50), channel_id=1, replica_groups=mesh['dp'=8,'tensor'=16] {'tensor'}, dimensions={0} | all-to-all | bytes 524288 | tf_op jit(solution)/shard_map/all_to_all | solution.py:14
  661.9 0.5 broadcast.68
  662.4 1.3 reduce.6
  663.7 0.2 reshape.51
  663.9 0.1 copy.29
  664.0 5.8 cholesky.16
  669.9 0.6 compare_reduce_fusion
  670.6 0.7 fusion.10
  671.2 4.9 custom-call.7
  676.1 0.3 fusion.6
  676.4 8.7 %convolution_multiply_fusion.2 = f32[5120,64]{0,1:T(8,128)} fusion(f32[256,5120]{0,1:T(8,128)} %copy-done.2, f32[64,256]{1,0:T(8,128)S(1)} %fusion.6), kind=kOutput, calls=%fused_computation.9 | convolution fusion | flops 1006960640 | bytes 6619136 | tf_op jit(solution)/shard_map/dot_general | solution.py:49
  685.1 0.0 all-reduce.2.cloned.1.call-update
  685.1 146.8 %all-reduce.2.cloned.1.call-done = f32[5120,64]{0,1:T(8,128)} async-done(((f32[5120,64]{0,1:T(8,128)}), f32[5120,64]{0,1:T(8,128)}) %all-reduce.2.cloned.1.call-update) | async-done | bytes 1310736 | tf_op jit(solution)/shard_map/psum | solution.py:50
  831.9 9.7 %fusion.2 = f32[1,256,5120]{1,2,0:T(8,128)} fusion(f32[256,5120]{0,1:T(8,128)} %copy-done.2, f32[64,256]{1,0:T(8,128)S(1)} %fusion.6, f32[5120,64]{0,1:T(8,128)} %all-reduce.2.cloned.1.call-done), kind=kOutput, calls=%fused_computation.4 | convolution fusion | flops 1009254400 | bytes 11862016 | tf_op jit(solution)/shard_map/dot_general | solution.py:53
  841.6 6.0 copy.31
  847.6 0.2 multiply_reduce_fusion
  847.8 0.2 broadcast_multiply_fusion.1
  848.0 1.4 copy-done.5
  849.4 5.8 fusion.3
  (23 shorter events, 0.3 us)
Async XLA Ops:
  7.2 601.4 %copy-start = (bf16[3072,256]{1,0:T(8,128)(2,1)S(1)}, bf16[3072,256]{1,0:T(8,128)(2,1)}, u32[]{:S(2)}) copy-start(bf16[3072,256]{1,0:T(8,128)(2,1)} %param.7) | copy-start | bytes 4718596
  20.4 588.2 %all-to-all-start = ((bf16[16,3072,320]{1,2,0:T(8,128)(2,1)}), bf16[16,3072,320]{1,2,0:T(8,128)(2,1)}, u32[]{:S(2)}, u32[]{:S(2)}) async-start(bf16[16,3072,320]{1,2,0:T(8,128)(2,1)} %stack.2), calls=%async_computation | async-start | bytes 62914560 | tf_op jit(solution)/shard_map/all_to_all | solution.py:33
  28.8 5.9 copy-start.7
  28.8 803.1 %all-reduce.2.cloned.1.call-start = ((), (), s32[]{:S(2)}) async-start(), calls=%async_computation.3 | async-start | bytes 2621440 | tf_op jit(solution)/shard_map/psum | solution.py:50
  608.5 17.1 %copy-start.6 = (f32[5120,64]{0,1:T(8,128)S(1)}, f32[5120,64]{0,1:T(8,128)}, u32[]{:S(2)}) copy-start(f32[5120,64]{0,1:T(8,128)} %param.11) | copy-start | bytes 3932164
  625.7 3.2 copy-start.2
  841.6 6.0 copy-start.3
  847.6 1.7 copy-start.5
  847.8 7.3 copy-start.1
  849.4 5.8 copy-start.4
Sparse Core Ops, SparseCore 0:
  685.2 146.6 all-reduce.1

commit v2 on v0

--- a/solution.py
+++ b/solution.py
@@ -39,7 +39,7 @@
     factor = jnp.linalg.cholesky(gram)
     ortho = jax.scipy.linalg.solve_triangular(factor, left.T, lower=True).T
     term = lax.dot_general(both, ortho, contract, precision=hi) / replicas
-    right = lax.psum(term, ("dp", "tensor"))
+    right = lax.psum(lax.psum(term, axis_name="tensor"), axis_name="dp")
     squares = jnp.sum(right * right, axis=0)
     new_right = right * lax.rsqrt(squares + EPS)
     lowrank = jnp.dot(ortho, right.T, precision=hi)

time: 450 us -> 454 us (level)
    psum x1 -> x2, waiting for transfers between devices: 147 us -> 149 us  [per_device(): right = lax.psum(lax.psum(term, axis_name='tensor'), axis_name='dp')]
  transfers between devices with their start and end apart: 2 -> 3, of which waited for: 2 -> 3; matrix products, arithmetic and copies ran while one was open for 1% -> 1% of each run, Pallas kernels for 0% -> 0%
where the time goes in v2:
time: 454 us; the launch traced here: 452 us
  waiting for transfers between devices  332 us (73%)
  matrix products  44.9 us (10%)
  blocking collectives  26.5 us (6%)
  other arithmetic  19.5 us (4%)
  local copies, waits for them, and re-layouts  14.7 us (3%)
  between operations  13.9 us (3%)
    all_gather x1, waiting for transfers between devices, per_device(): lax.all_gather(masked, 'tensor', axis=1, tiled=True)  183 us
    psum x2, waiting for transfers between devices, per_device(): right = lax.psum(lax.psum(term, axis_name='tensor'), axis_name='dp')  149 us
    all_to_all x2, blocking collectives, from_everyone(): lax.all_to_all(jnp.broadcast_to(x[None], (devices, *x.shape)), axis, 0, 0...  26.5 us
    dot_general x1, matrix products, per_device(): lax.dot_general(cotangent, lax.all_gather(masked, 'tensor', axis=1, tiled...  17.1 us
    unnamed x20, local copies, waits for them, and re-layouts  14 us
    dot_general x1, matrix products, per_device(): lowrank = jnp.dot(ortho, right.T, precision=hi)  9.7 us
  transfers between devices with their start and end apart: 3, of which 3 were waited for; matrix products, arithmetic and copies ran while one was open for 1% of the time, Pallas kernels for 0%

profile of v2, /device:TPU:1, one launch (start us, length us, event | category | flops | bytes accessed | tf_op | source)
XLA Modules:
  0.0 451.8 jit_solution(1180807725015690461)
XLA Ops:
  7.2 0.0 all-gather.2.cloned.1.call-start
  7.2 0.8 fusion.15
  8.1 3.0 broadcast_multiply_fusion
  11.1 0.0 all-reduce.3.cloned.1.call-start
  11.1 5.9 %copy.22 = f32[1,256,5120]{1,2,0:T(8,128)} copy(f32[1,256,5120]{2,1,0:T(8,128)} %param.9) | data formatting | bytes 10485760 | tf_op args[3]
  17.0 0.6 convert_reduce_fusion
  17.6 183.0 %all-gather.2.cloned.1.call-done = bf16[3072,5120]{0,1:T(8,128)(2,1)} async-done(((bf16[3072,320]{0,1:T(8,128)(2,1)}), bf16[3072,5120]{0,1:T(8,128)(2,1)}) %all-gather.2.cloned.1.call-update) | async-done | bytes 31457296 | tf_op jit(solution)/shard_map/all_gather | solution.py:32
  200.6 17.1 %fusion.5 = f32[256,5120]{0,1:T(8,128)S(1)} fusion(bf16[3072,5120]{0,1:T(8,128)(2,1)} %all-gather.2.cloned.1.call-done, bf16[3072,256]{1,0:T(8,128)(2,1)S(1)} %copy-done, f32[1,256,5120]{1,2,0:T(8,128)} %copy.22, f32[]{:T(128)} %convert_reduce_fusion), kind=kOutput, calls=%fused_computation.8 | convolution fusion | flops 8055685120 | bytes 43515908 | tf_op jit(solution)/shard_map/dot_general | solution.py:30
  217.7 3.2 fusion.18
  221.0 14.2 %all_to_all.10 = f32[8,256,64]{1,2,0:T(8,128)S(1)} all-to-all(f32[8,256,64]{1,2,0:T(8,128)S(1)} %broadcast_in_dim.7), channel_id=1, replica_groups=mesh['dp'=8,'tensor'=16] {'dp'}, dimensions={0} | all-to-all | bytes 1048576 | tf_op jit(solution)/shard_map/all_to_all | solution.py:14
  235.2 0.2 fusion.8
  235.5 0.3 reshape.40
  235.8 12.2 %all_to_all.11 = f32[16,1,4096]{2,1,0:T(1,128)S(1)} all-to-all(f32[16,1,4096]{2,1,0:T(1,128)S(1)} %reshape.40), channel_id=1, replica_groups=mesh['dp'=8,'tensor'=16] {'tensor'}, dimensions={0} | all-to-all | bytes 524288 | tf_op jit(solution)/shard_map/all_to_all | solution.py:14
  248.1 0.5 broadcast.66
  248.6 1.3 reduce.6
  249.8 0.2 reshape.41
  250.1 0.1 copy.23
  250.2 5.8 %cholesky.16 = f32[64,64]{1,0:T(8,128)S(1)} custom-call(f32[64,64]{1,0:T(8,128)S(1)} %fusion.12), custom_call_target="Cholesky" | custom-call | tf_op jit(solution)/shard_map/jit(cholesky)/cholesky | solution.py:39
  256.1 0.6 compare_reduce_fusion
  256.7 0.7 fusion.10
  257.4 4.9 %custom-call.7 = f32[1,64,64]{1,2,0:T(8,128)S(1)} custom-call(f32[1,64,64]{2,1,0:T(8,128)S(1)} %fusion.10), custom_call_target="InvertDiagBlocksLowerTriangular" | custom-call | tf_op jit(solution)/shard_map/jit(_solve_triangular)/triangular_solve | solution.py:40
  262.3 0.3 fusion.6
  262.6 8.7 %convolution_multiply_fusion.2 = f32[5120,64]{0,1:T(8,128)} fusion(f32[256,5120]{0,1:T(8,128)} %copy-done.2, f32[64,256]{1,0:T(8,128)S(1)} %fusion.6), kind=kOutput, calls=%fused_computation.9 | convolution fusion | flops 1006960640 | bytes 6619136 | tf_op jit(solution)/shard_map/dot_general | solution.py:41
  271.3 0.3 all-reduce.5.cloned.1.call-start
  271.6 84.4 %all-reduce.3.cloned.1.call-done = f32[5120,64]{0,1:T(8,128)} async-done(((f32[5120,64]{0,1:T(8,128)}), f32[5120,64]{0,1:T(8,128)}) %all-reduce.3.cloned.1.call-update) | async-done | bytes 1310736 | tf_op jit(solution)/shard_map/psum | solution.py:42
  356.0 64.6 %all-reduce.5.cloned.1.call-done = f32[5120,64]{0,1:T(8,128)} async-done(((f32[5120,64]{0,1:T(8,128)}), f32[5120,64]{0,1:T(8,128)}) %all-reduce.5.cloned.1.call-update) | async-done | bytes 1310736 | tf_op jit(solution)/shard_map/psum | solution.py:42
  420.5 1.5 multiply_reduce_fusion
  422.0 9.7 %fusion.2 = f32[1,256,5120]{1,2,0:T(8,128)} fusion(f32[256,5120]{0,1:T(8,128)} %copy-done.2, f32[64,256]{1,0:T(8,128)S(1)} %fusion.6, f32[5120,64]{0,1:T(8,128)} %all-reduce.5.cloned.1.call-done), kind=kOutput, calls=%fused_computation.4 | convolution fusion | flops 1009254400 | bytes 11862016 | tf_op jit(solution)/shard_map/dot_general | solution.py:45
  431.7 6.0 %copy.25 = f32[1,256,5120]{2,1,0:T(8,128)} copy(f32[1,256,5120]{1,2,0:T(8,128)} %fusion.2) | data formatting | bytes 10485760
  437.7 0.2 broadcast_multiply_fusion.1
  437.9 1.6 copy-done.5
  439.5 5.8 %fusion.3 = bf16[256,5120]{1,0:T(8,128)(2,1)} fusion(f32[64,256]{1,0:T(8,128)S(1)} %fusion.6, f32[5120,64]{0,1:T(8,128)S(1)} %broadcast_multiply_fusion.1, bf16[256,5120]{1,0:T(8,128)(2,1)S(1)} %copy-done.5), kind=kOutput, calls=%fused_computation.5 | convolution fusion | flops 1011875840 | bytes 6619136 | tf_op jit(solution)/shard_map/dot_general | solution.py:48
  (26 shorter events, 0.3 us)
Async XLA Ops:
  7.2 193.5 %copy-start = (bf16[3072,256]{1,0:T(8,128)(2,1)S(1)}, bf16[3072,256]{1,0:T(8,128)(2,1)}, u32[]{:S(2)}) copy-start(bf16[3072,256]{1,0:T(8,128)(2,1)} %param.7) | copy-start | bytes 4718596
  7.2 193.5 %all-gather.2.cloned.1.call-start = ((), (), s32[]{:S(2)}) async-start(), calls=%async_computation.2 | async-start | bytes 33423360 | tf_op jit(solution)/shard_map/all_gather | solution.py:32
  11.1 5.9 %copy-start.7 = (s32[8]{0:T(128)S(1)}, s32[8]{0:T(128)}, u32[]{:S(2)}) copy-start(s32[8]{0:T(128)} %param.8) | copy-start | bytes 100
  11.1 344.9 %all-reduce.3.cloned.1.call-start = ((), (), s32[]{:S(2)}) async-start(), calls=%async_computation.3 | async-start | bytes 2621440 | tf_op jit(solution)/shard_map/psum | solution.py:42
  17.6 200.1 %copy-start.6 = (f32[5120,64]{0,1:T(8,128)S(1)}, f32[5120,64]{0,1:T(8,128)}, u32[]{:S(2)}) copy-start(f32[5120,64]{0,1:T(8,128)} %param.11) | copy-start | bytes 3932164
  217.7 3.2 copy-start.2
  271.3 149.2 %all-reduce.5.cloned.1.call-start = ((), (), s32[]{:S(2)}) async-start(), calls=%async_computation.4 | async-start | bytes 2621440 | tf_op jit(solution)/shard_map/psum | solution.py:42
  431.7 6.0 %copy-start.3 = (f32[5120,64]{0,1:T(8,128)S(1)}, f32[5120,64]{0,1:T(8,128)}, u32[]{:S(2)}) copy-start(f32[5120,64]{0,1:T(8,128)} %all-reduce.5.cloned.1.call-done) | copy-start | bytes 3932164
  437.7 1.7 copy-start.5
  437.7 7.6 %copy-start.1 = (bf16[3072,256]{1,0:T(8,128)(2,1)S(1)}, bf16[3072,256]{1,0:T(8,128)(2,1)}, u32[]{:S(2)}) copy-start(bf16[3072,256]{1,0:T(8,128)(2,1)} %param.7) | copy-start | bytes 4718596
  439.5 5.8 %copy-start.4 = (f32[5120,64]{0,1:T(8,128)}, f32[5120,64]{0,1:T(8,128)S(1)}, u32[]{:S(2)}) copy-start(f32[5120,64]{0,1:T(8,128)S(1)} %broadcast_multiply_fusion.1) | copy-start | bytes 3932164
Sparse Core Ops, SparseCore 0:
  11.2 189.4 all-gather.1
  271.4 84.4 all-reduce.2
  358.3 62.1 all-reduce.4
